TPU v7x, 128 devices: a whole 4x4x4 slice. The times are simulated.
128 devices in a mesh: tm: 128 (over z, y, x, core).
Axes of the slice: x: 4, y: 4, z: 4, core: 2. Of those that a mesh axis runs over, the one named last changes fastest.
Arguments:
- krylov_basis: float32 [8, 512, 32, 512], P(None, 'tm'), may hold values from -6 to 6, as said below
- vector: float32 [512, 32, 512], P('tm'), may hold values from -60 to 60
- conductance: float32 [32, 512], replicated, may hold values from 1e-05 to 0.3
Outputs:
- preconditioned: float32 [512, 32, 512], P('tm')
- next_vector: float32 [512, 32, 512], P('tm')
- coefficients: float32 [9], replicated
Inputs may be any that keep to these rules, and one draw needn't show every extreme that they name: `krylov_basis`: the 8 fields are orthonormal, up to float32 rounding, under the mean over all cells of their product.
All inputs are finite; a program needn't handle non-finite values.
Results may differ from a plain program's by a relative error of at most 0.0003.
Values sent between devices are 32-bit elements.
No kernel may reach another device: no remote copies, remote signals or barrier semaphores. Data moves between devices by JAX's collectives and lax.ppermute only.
A program may use at most 64 MiB of HBM per device.

v0:
```python
import functools

import jax
import jax.numpy as jnp
from jax import lax
from jax.sharding import Mesh
from jax.sharding import PartitionSpec as P

LEVELS = 3
TM = ("tm_0", "tm_1", "tm_2", "tm_3")


OMEGA = 0.7
FLOOR = 0.25


def passed_along(value, axis, steps):
    count = lax.axis_size(axis)
    initial, last = (max(0, -steps), min(count, count - steps))
    return lax.ppermute(value, axis, [(source, source + steps) for source in range(initial, last)])


def nothing_yet(value, identity):
    return jax.tree.map(
        lambda a, e: jnp.broadcast_to(jnp.asarray(e, a.dtype), a.shape), value, identity
    )


def carried_in(value, axes, combine, identity):
    before = start = nothing_yet(value, identity)
    subtotal = value
    for axis in reversed(axes):
        length, mine = (lax.axis_size(axis), lax.axis_index(axis))
        pieces = jax.tree.map(lambda part: lax.all_gather(part, axis), subtotal)
        inside, subtotal = (start, start)
        for k in range(length):
            passed = k < mine
            subtotal = combine(subtotal, jax.tree.map(lambda part: part[k], pieces))
            inside = jax.tree.map(lambda new, old: jnp.where(passed, new, old), subtotal, inside)
        before = combine(inside, before)
    return before


def by_axis(value, axes):
    return functools.reduce(lax.psum, axes, value)


def beside(volume):
    padded = jnp.pad(volume, ((0, 0), (1, 1), (1, 1)))
    return padded[:, 2:, 1:-1] + padded[:, :-2, 1:-1] + padded[:, 1:-1, 2:] + padded[:, 1:-1, :-2]


def spatial(volume, conduct):
    return volume + conduct * (4.0 * volume - beside(volume))


def time_operator(volume, conduct):
    incoming = passed_along(volume[-1], TM, 1)
    earlier = jnp.concatenate([incoming[None], volume[:-1]], axis=0)
    return spatial(volume, conduct) - earlier


def block_inverse(source, conduct):
    diagonal = 1.0 + 4.0 * conduct
    sweep_one = source / diagonal
    return (source + conduct * beside(sweep_one)) / diagonal


def march_from(entry, source, diagonal):

    def advance(carry_state, slab_in):
        carry_state = (slab_in + carry_state) / diagonal
        return (carry_state, carry_state)

    return lax.scan(advance, entry, source)[1]


def coarse_solve(source, conduct):
    diagonal = 1.0 + 4.0 * conduct
    nothing = jnp.zeros_like(conduct)
    partial_march = march_from(nothing, source, diagonal)
    slabs = source.shape[0]
    damping = 1.0 / diagonal
    factor = damping**slabs

    def combine_pair(earlier, following):
        return (earlier[0] * following[0], following[0] * earlier[1] + following[1])

    carried = carried_in(
        (factor, partial_march[-1]), TM, combine_pair, (jnp.ones_like(conduct), nothing)
    )
    entry = carried[1]
    return march_from(entry, source, diagonal)


def vcycle(source, conduct, level_at):
    if level_at == LEVELS - 1:
        return coarse_solve(source, conduct)
    smooth = OMEGA * block_inverse(source, conduct)
    remain = source - time_operator(smooth, conduct)
    coarse = remain[0::2] + remain[1::2]
    correction = vcycle(coarse, 2.0 * conduct, level_at + 1)
    smooth = smooth + jnp.repeat(correction, 2, axis=0)
    return smooth + OMEGA * block_inverse(source - time_operator(smooth, conduct), conduct)


def on_device(krylov_basis, vector, conductance):
    count_all = vector.shape[0] * lax.axis_size(TM) * vector.shape[1] * vector.shape[2]
    preconditioned = vcycle(vector, conductance, 0)
    applied = time_operator(preconditioned, conductance)
    partial_dots = jnp.einsum("kabc,abc->k", krylov_basis, applied, precision=lax.Precision.HIGHEST)
    weights = by_axis(partial_dots, TM) / count_all
    applied = applied - jnp.einsum(
        "k,kabc->abc", weights, krylov_basis, precision=lax.Precision.HIGHEST
    )
    length = jnp.sqrt(by_axis(jnp.sum(applied * applied), TM) / count_all)
    next_vector = applied / jnp.maximum(length, FLOOR)
    coefficients = jnp.concatenate([weights, length[None]])
    return (preconditioned, next_vector, coefficients)


def solution(mesh):
    split = Mesh(mesh.devices.reshape(4, 4, 4, 2), ("tm_0", "tm_1", "tm_2", "tm_3"))
    return jax.shard_map(
        on_device,
        mesh=split,
        in_specs=(P(None, TM, None, None), P(TM, None, None), P()),
        out_specs=(P(TM, None, None), P(TM, None, None), P()),
        check_vma=False,
    )
```

profile of v0, /device:TPU:1, one launch (start us, length us, event | category | flops | bytes accessed | tf_op | source)
XLA Modules:
  0.0 206.2 jit_solution(512129045532581927)
XLA Ops:
  3.8 4.5 %collective-permute-start = (f32[32,512]{1,0:T(8,128)S(1)}, f32[32,512]{1,0:T(8,128)S(1)}, u32[]{:S(2)}, u32[]{:S(2)}) collective-permute-start(f32[32,512]{1,0:T(8,128)S(1)} %slice_bitcast_fusion.4), channel_id=1, source_target_pairs={{0,1},{1,2},{2,3},{3,4},{4,5},{5,6},{6,7},{7,8},{8,9},{9,10},{10,1... | collective-permute-start | bytes 196616 | tf_op jit(solution)/shard_map/ppermute | solution.py:20
  10.1 4.3 %collective-permute-start.1 = (f32[32,512]{1,0:T(8,128)S(1)}, f32[32,512]{1,0:T(8,128)S(1)}, u32[]{:S(2)}, u32[]{:S(2)}) collective-permute-start(f32[32,512]{1,0:T(8,128)S(1)} %get-tuple-element.51), channel_id=1, source_target_pairs={{0,1},{1,2},{2,3},{3,4},{4,5},{5,6},{6,7},{7,8},{8,9},{9,10},{10,1... | collective-permute-start | bytes 196616 | tf_op jit(solution)/shard_map/ppermute | solution.py:20
  15.9 1.9 all-gather
  17.8 1.9 all-gather.1
  19.7 12.0 %all_gather.35 = f32[4,32,512]{2,1,0:T(8,128)S(1)} all-gather(f32[1,32,512]{2,1,0:T(8,128)S(1)} %get-tuple-element.49), channel_id=1, replica_groups=mesh['tm_0'=4,'tm_1'=4,'tm_2'=4,'tm_3'=2] {'tm_2'}, dimensions={0}, use_global_device_ids=true | all-gather | bytes 327680 | tf_op jit(solution)/shard_map/all_gather | solution.py:34
  31.7 9.4 %all_gather.39 = f32[4,32,512]{2,1,0:T(8,128)S(1)} all-gather(f32[1,32,512]{2,1,0:T(8,128)S(1)} %get-tuple-element.50), channel_id=1, replica_groups=mesh['tm_0'=4,'tm_1'=4,'tm_2'=4,'tm_3'=2] {'tm_2'}, dimensions={0}, use_global_device_ids=true | all-gather | bytes 327680 | tf_op jit(solution)/shard_map/all_gather | solution.py:34
  41.1 13.3 %all_gather.36 = f32[4,32,512]{2,1,0:T(8,128)S(1)} all-gather(f32[1,32,512]{2,1,0:T(8,128)S(1)} %get-tuple-element.45), channel_id=1, replica_groups=mesh['tm_0'=4,'tm_1'=4,'tm_2'=4,'tm_3'=2] {'tm_1'}, dimensions={0}, use_global_device_ids=true | all-gather | bytes 327680 | tf_op jit(solution)/shard_map/all_gather | solution.py:34
  54.3 9.4 %all_gather.40 = f32[4,32,512]{2,1,0:T(8,128)S(1)} all-gather(f32[1,32,512]{2,1,0:T(8,128)S(1)} %get-tuple-element.46), channel_id=1, replica_groups=mesh['tm_0'=4,'tm_1'=4,'tm_2'=4,'tm_3'=2] {'tm_1'}, dimensions={0}, use_global_device_ids=true | all-gather | bytes 327680 | tf_op jit(solution)/shard_map/all_gather | solution.py:34
  63.7 14.6 %all_gather.37 = f32[4,32,512]{2,1,0:T(8,128)S(1)} all-gather(f32[1,32,512]{2,1,0:T(8,128)S(1)} %get-tuple-element.43), channel_id=1, replica_groups=mesh['tm_0'=4,'tm_1'=4,'tm_2'=4,'tm_3'=2] {'tm_0'}, dimensions={0}, use_global_device_ids=true | all-gather | bytes 327680 | tf_op jit(solution)/shard_map/all_gather | solution.py:34
  78.4 9.4 %all_gather.41 = f32[4,32,512]{2,1,0:T(8,128)S(1)} all-gather(f32[1,32,512]{2,1,0:T(8,128)S(1)} %get-tuple-element.44), channel_id=1, replica_groups=mesh['tm_0'=4,'tm_1'=4,'tm_2'=4,'tm_3'=2] {'tm_0'}, dimensions={0}, use_global_device_ids=true | all-gather | bytes 327680 | tf_op jit(solution)/shard_map/all_gather | solution.py:34
  88.0 17.1 %collective-permute-start.2 = (f32[32,512]{1,0:T(8,128)S(1)}, f32[32,512]{1,0:T(8,128)S(1)}, u32[]{:S(2)}, u32[]{:S(2)}) collective-permute-start(f32[32,512]{1,0:T(8,128)S(1)} %get-tuple-element.47), channel_id=1, source_target_pairs={{0,1},{1,2},{2,3},{3,4},{4,5},{5,6},{6,7},{7,8},{8,9},{9,10},{10,1... | collective-permute-start | bytes 196616 | tf_op jit(solution)/shard_map/ppermute | solution.py:20
  105.1 1.5 collective-permute-done.2
  107.0 4.1 %collective-permute-start.3 = (f32[32,512]{1,0:T(8,128)S(1)}, f32[32,512]{1,0:T(8,128)S(1)}, u32[]{:S(2)}, u32[]{:S(2)}) collective-permute-start(f32[32,512]{1,0:T(8,128)S(1)} %slice_bitcast_fusion.1), channel_id=1, source_target_pairs={{0,1},{1,2},{2,3},{3,4},{4,5},{5,6},{6,7},{7,8},{8,9},{9,10},{10,1... | collective-permute-start | bytes 196616 | tf_op jit(solution)/shard_map/ppermute | solution.py:20
  112.8 4.3 %collective-permute-start.4 = (f32[32,512]{1,0:T(8,128)S(1)}, f32[32,512]{1,0:T(8,128)S(1)}, u32[]{:S(2)}, u32[]{:S(2)}) collective-permute-start(f32[32,512]{1,0:T(8,128)S(1)} %slice_bitcast_fusion), channel_id=1, source_target_pairs={{0,1},{1,2},{2,3},{3,4},{4,5},{5,6},{6,7},{7,8},{8,9},{9,10},{10,1... | collective-permute-start | bytes 196616 | tf_op jit(solution)/shard_map/ppermute | solution.py:20
  118.6 5.3 %fusion.4 = f32[8]{0:T(128)S(1)} fusion(f32[8,4,32,512]{3,2,1,0:T(8,128)S(1)} %copy-done, f32[4,32,512,1]{2,1,0,3:T(8,128)S(1)} %bitcast.206), kind=kOutput, calls=%fused_computation.4 | convolution fusion | flops 6291456 | bytes 2359328 | tf_op jit(solution)/shard_map/kabc,abc->k/dot_general | solution.py:111
  124.0 17.8 %psum.56 = f32[8]{0:T(128)S(1)} all-reduce(f32[8]{0:T(128)S(1)} %fusion.4), channel_id=1, replica_groups=mesh['tm_0'=4,'tm_1'=4,'tm_2'=4,'tm_3'=2] {'tm_0'}, use_global_device_ids=true, to_apply=%region_0.1 | all-reduce | flops 8 | bytes 64 | tf_op jit(solution)/shard_map/psum | solution.py:45
  141.8 6.0 %psum.57 = f32[8]{0:T(128)S(1)} all-reduce(f32[8]{0:T(128)S(1)} %psum.56), channel_id=1, replica_groups=mesh['tm_0'=4,'tm_1'=4,'tm_2'=4,'tm_3'=2] {'tm_1'}, use_global_device_ids=true, to_apply=%region_1.2 | all-reduce | flops 8 | bytes 64 | tf_op jit(solution)/shard_map/psum | solution.py:45
  147.8 10.0 %psum.58 = f32[8]{0:T(128)S(1)} all-reduce(f32[8]{0:T(128)S(1)} %psum.57), channel_id=1, replica_groups=mesh['tm_0'=4,'tm_1'=4,'tm_2'=4,'tm_3'=2] {'tm_2'}, use_global_device_ids=true, to_apply=%region_2.3 | all-reduce | flops 8 | bytes 64 | tf_op jit(solution)/shard_map/psum | solution.py:45
  157.8 10.7 %psum.59 = f32[8]{0:T(128)S(1)} all-reduce(f32[8]{0:T(128)S(1)} %psum.58), channel_id=1, replica_groups=mesh['tm_0'=4,'tm_1'=4,'tm_2'=4,'tm_3'=2] {'tm_3'}, use_global_device_ids=true, to_apply=%region_3.4 | all-reduce | flops 8 | bytes 64 | tf_op jit(solution)/shard_map/psum | solution.py:45
  168.5 2.8 %fusion = f32[1,4,32,512]{3,0,2,1:T(1,128)S(1)} fusion(f32[8,4,32,512]{3,2,1,0:T(8,128)S(1)} %copy-done, f32[8]{0:T(128)S(1)} %psum.59), kind=kOutput, calls=%fused_computation | convolution fusion | flops 6291464 | bytes 2359328 | tf_op jit(solution)/shard_map/k,kabc->abc/dot_general | solution.py:113
  172.0 6.7 %psum.60 = f32[]{:T(128)} all-reduce(f32[]{:T(128)} %multiply_reduce_fusion), channel_id=1, replica_groups=mesh['tm_0'=4,'tm_1'=4,'tm_2'=4,'tm_3'=2] {'tm_0'}, use_global_device_ids=true, to_apply=%region_5.6 | all-reduce | flops 1 | bytes 8 | tf_op jit(solution)/shard_map/psum | solution.py:45
  178.7 8.3 %psum.61 = f32[]{:T(128)} all-reduce(f32[]{:T(128)} %psum.60), channel_id=1, replica_groups=mesh['tm_0'=4,'tm_1'=4,'tm_2'=4,'tm_3'=2] {'tm_1'}, use_global_device_ids=true, to_apply=%region_6.7 | all-reduce | flops 1 | bytes 8 | tf_op jit(solution)/shard_map/psum | solution.py:45
  187.1 8.3 %psum.62 = f32[]{:T(128)} all-reduce(f32[]{:T(128)} %psum.61), channel_id=1, replica_groups=mesh['tm_0'=4,'tm_1'=4,'tm_2'=4,'tm_3'=2] {'tm_2'}, use_global_device_ids=true, to_apply=%region_7.8 | all-reduce | flops 1 | bytes 8 | tf_op jit(solution)/shard_map/psum | solution.py:45
  195.4 8.7 %psum.63 = f32[]{:T(128)} all-reduce(f32[]{:T(128)} %psum.62), channel_id=1, replica_groups=mesh['tm_0'=4,'tm_1'=4,'tm_2'=4,'tm_3'=2] {'tm_3'}, use_global_device_ids=true, to_apply=%region_8.9 | all-reduce | flops 1 | bytes 8 | tf_op jit(solution)/shard_map/psum | solution.py:45
  (43 shorter events, 12.3 us)
Async XLA Ops:
  0.6 118.0 %copy-start = (f32[8,4,32,512]{3,2,1,0:T(8,128)S(1)}, f32[8,4,32,512]{3,2,1,0:T(8,128)}, u32[]{:S(2)}) copy-start(f32[8,4,32,512]{3,2,1,0:T(8,128)} %param.3) | copy-start | bytes 6291460
  0.6 9.0 %copy-start.2 = (f32[32,512]{1,0:T(8,128)S(1)}, f32[32,512]{1,0:T(8,128)}, u32[]{:S(2)}) copy-start(f32[32,512]{1,0:T(8,128)} %param.5) | copy-start | bytes 196612
  0.7 9.0 %copy-start.1 = (f32[4,32,512]{2,1,0:T(8,128)S(1)}, f32[4,32,512]{2,1,0:T(8,128)}, u32[]{:S(2)}) copy-start(f32[4,32,512]{2,1,0:T(8,128)} %param.4) | copy-start | bytes 786436
  3.8 5.8 %collective-permute-start = (f32[32,512]{1,0:T(8,128)S(1)}, f32[32,512]{1,0:T(8,128)S(1)}, u32[]{:S(2)}, u32[]{:S(2)}) collective-permute-start(f32[32,512]{1,0:T(8,128)S(1)} %slice_bitcast_fusion.4), channel_id=1, source_target_pairs={{0,1},{1,2},{2,3},{3,4},{4,5},{5,6},{6,7},{7,8},{8,9},{9,10},{10,1... | collective-permute-start | bytes 196616 | tf_op jit(solution)/shard_map/ppermute | solution.py:20
  10.1 5.6 %collective-permute-start.1 = (f32[32,512]{1,0:T(8,128)S(1)}, f32[32,512]{1,0:T(8,128)S(1)}, u32[]{:S(2)}, u32[]{:S(2)}) collective-permute-start(f32[32,512]{1,0:T(8,128)S(1)} %get-tuple-element.51), channel_id=1, source_target_pairs={{0,1},{1,2},{2,3},{3,4},{4,5},{5,6},{6,7},{7,8},{8,9},{9,10},{10,1... | collective-permute-start | bytes 196616 | tf_op jit(solution)/shard_map/ppermute | solution.py:20
  88.0 18.6 %collective-permute-start.2 = (f32[32,512]{1,0:T(8,128)S(1)}, f32[32,512]{1,0:T(8,128)S(1)}, u32[]{:S(2)}, u32[]{:S(2)}) collective-permute-start(f32[32,512]{1,0:T(8,128)S(1)} %get-tuple-element.47), channel_id=1, source_target_pairs={{0,1},{1,2},{2,3},{3,4},{4,5},{5,6},{6,7},{7,8},{8,9},{9,10},{10,1... | collective-permute-start | bytes 196616 | tf_op jit(solution)/shard_map/ppermute | solution.py:20
  107.0 5.4 %collective-permute-start.3 = (f32[32,512]{1,0:T(8,128)S(1)}, f32[32,512]{1,0:T(8,128)S(1)}, u32[]{:S(2)}, u32[]{:S(2)}) collective-permute-start(f32[32,512]{1,0:T(8,128)S(1)} %slice_bitcast_fusion.1), channel_id=1, source_target_pairs={{0,1},{1,2},{2,3},{3,4},{4,5},{5,6},{6,7},{7,8},{8,9},{9,10},{10,1... | collective-permute-start | bytes 196616 | tf_op jit(solution)/shard_map/ppermute | solution.py:20
  112.8 58.5 %copy-start.3 = (f32[4,32,512]{2,1,0:T(8,128)}, f32[4,32,512]{2,1,0:T(8,128)S(1)}, u32[]{:S(2)}) copy-start(f32[4,32,512]{2,1,0:T(8,128)S(1)} %multiply_add_fusion) | copy-start | bytes 786436
  112.8 5.6 %collective-permute-start.4 = (f32[32,512]{1,0:T(8,128)S(1)}, f32[32,512]{1,0:T(8,128)S(1)}, u32[]{:S(2)}, u32[]{:S(2)}) collective-permute-start(f32[32,512]{1,0:T(8,128)S(1)} %slice_bitcast_fusion), channel_id=1, source_target_pairs={{0,1},{1,2},{2,3},{3,4},{4,5},{5,6},{6,7},{7,8},{8,9},{9,10},{10,1... | collective-permute-start | bytes 196616 | tf_op jit(solution)/shard_map/ppermute | solution.py:20
where the time goes:
time: 207 us; the launch traced here: 206 us
  blocking collectives  148 us (71%)
  starting transfers between devices  34.2 us (17%)
  matrix products  8.17 us (4%)
  other arithmetic  7.01 us (3%)
  waiting for transfers between devices  6.65 us (3%)
    psum x8, blocking collectives, by_axis(): return functools.reduce(lax.psum, axes, value)  76.6 us
    all_gather x8, blocking collectives, carried_in(): pieces = jax.tree.map(lambda part: lax.all_gather(part, axis), subtotal)  71.7 us
    ppermute x5, starting transfers between devices, passed_along(): lax.ppermute(value, axis, [(source, source + steps) for source in range(i...  34.2 us
    ppermute x5, waiting for transfers between devices, passed_along(): lax.ppermute(value, axis, [(source, source + steps) for source in range(i...  6.65 us
    dot_general x1, matrix products, on_device(): jnp.einsum('kabc,abc->k', krylov_basis, applied, precision=lax.Precision....  5.33 us
  transfers between devices with their start and end apart: 5, of which 5 were waited for; matrix products, arithmetic and copies ran while one was open for 0% of the time, Pallas kernels for 0%

commit v1 on v0

v1 whole, which is shorter than its diff:
```python
import functools

import jax
import jax.numpy as jnp
from jax import lax
from jax.experimental import pallas as pl
from jax.experimental.pallas import tpu as pltpu
from jax.sharding import PartitionSpec as P

TM = "tm"
OMEGA = 0.7
FLOOR = 0.25
ROWS, LANES = 8, 128
VMEM = pltpu.VMEM


class Grid:
    def __init__(self, conduct):
        sx, sy = conduct.shape
        row = lax.broadcasted_iota(jnp.int32, (sx, sy), 0)
        col = lax.broadcasted_iota(jnp.int32, (sx, sy), 1)
        self.sx, self.sy = sx, sy
        self.first_row, self.last_row = row == 0, row == sx - 1
        self.first_col, self.last_col = col == 0, col == sy - 1
        self.conduct = conduct

    def beside(self, v):
        zero = jnp.zeros_like(v)
        above = jnp.where(self.first_row, zero, pltpu.roll(v, 1, 0))
        below = jnp.where(self.last_row, zero, pltpu.roll(v, self.sx - 1, 0))
        left = jnp.where(self.first_col, zero, pltpu.roll(v, 1, 1))
        right = jnp.where(self.last_col, zero, pltpu.roll(v, self.sy - 1, 1))
        return (above + below) + (left + right)

    def level(self, scale):
        return Level(self, scale)


class Level:
    def __init__(self, grid, scale):
        self.grid = grid
        self.c = scale * grid.conduct
        self.diag = 1.0 + 4.0 * self.c
        self.inv = 1.0 / self.diag
        self.winv = OMEGA * self.inv

    def K(self, v):
        return self.diag * v - self.c * self.grid.beside(v)

    def S(self, r):
        return (r + self.c * self.grid.beside(r * self.inv)) * self.winv

    def T(self, v):
        return v + self.S(v - self.K(v))


def tiles(sx, sy):
    for i in range(sx // ROWS):
        for l in range(sy // LANES):
            yield (i * (sy // LANES) + l), slice(ROWS * i, ROWS * (i + 1)), slice(LANES * l, LANES * (l + 1))


def down_kernel(r_ref, c_ref, f_ref, d_ref, halo_ref, x_ref, keep_ref, ct_ref):
    sx, sy = c_ref.shape
    grid = Grid(c_ref[...])
    fine, mid = grid.level(1.0), grid.level(2.0)
    diag2 = 1.0 + 16.0 * c_ref[...]
    r = [r_ref[t] for t in range(4)]
    u = [fine.S(r[t]) for t in range(4)]
    rho0 = r[0] + r[1] - fine.K(u[0] + u[1]) + u[0]
    rho1 = r[2] + r[3] - fine.K(u[2] + u[3]) + u[1] + u[2]
    x = u[3]
    v0 = mid.S(rho0)
    v1 = mid.S(rho1)
    vs = v0 + v1
    loc = rho0 + rho1 - mid.K(vs) + v0
    sx_ = mid.S(x)
    g = x + v1 + sx_ - mid.K(sx_)
    f = loc / diag2 + g
    for t, rows, cols in tiles(sx, sy):
        f_ref[t * ROWS : (t + 1) * ROWS, :] = f[rows, cols]
        ct_ref[t * ROWS : (t + 1) * ROWS, :] = c_ref[rows, cols]
    me = lax.axis_index(TM)
    d_ref[...] = 1.0 / (1.0 + 16.0 * ct_ref[pl.ds(me, 1), :])
    alpha = v1 + mid.S(rho1 - mid.K(v1) + v0) - mid.T(g)
    beta = x + fine.S(r[3] - fine.K(x) + u[2])
    halo_ref[0] = x
    halo_ref[1] = alpha
    halo_ref[2] = beta
    x_ref[...] = x
    for t in range(4):
        keep_ref[t] = u[t]
    keep_ref[4] = rho0
    keep_ref[5] = rho1
    keep_ref[6] = loc


def scan_kernel(f_ref, d_ref, e_ref):
    count = f_ref.shape[0]
    row = lax.broadcasted_iota(jnp.int32, (ROWS, LANES), 0)
    d1 = jnp.broadcast_to(d_ref[...], (ROWS, LANES))
    d2 = d1 * d1
    d4 = d2 * d2
    d8 = d4 * d4
    one = jnp.ones_like(d1)
    power = (
        jnp.where((row & 1) > 0, d1, one)
        * jnp.where((row & 2) > 0, d2, one)
        * jnp.where((row & 4) > 0, d4, one)
    )
    carry = jnp.zeros((ROWS, LANES), jnp.float32)

    def shifted(v, by):
        return jnp.where(row < by, 0.0, pltpu.roll(v, by, 0))

    blocks = []
    for b in range(count // ROWS):
        y = f_ref[b * ROWS : (b + 1) * ROWS, :]
        y = y + d1 * shifted(y, 1)
        y = y + d2 * shifted(y, 2)
        y = y + d4 * shifted(y, 4)
        blocks.append(y)
    for b, y in enumerate(blocks):
        e_ref[b * ROWS : (b + 1) * ROWS, :] = shifted(y, 1) + power * carry
        carry = jnp.broadcast_to(y[ROWS - 1 : ROWS, :], (ROWS, LANES)) + d8 * carry


def up_kernel(e_ref, r_ref, c_ref, halo_ref, far_ref, keep_ref, q_hbm, p_ref, w_ref, dots_ref, q_ref, ef_ref, sem):
    copy = pltpu.make_async_copy(q_hbm, q_ref, sem)
    copy.start()
    sx, sy = c_ref.shape
    for t, rows, cols in tiles(sx, sy):
        ef_ref[rows, cols] = e_ref[t * ROWS : (t + 1) * ROWS, :]
    grid = Grid(c_ref[...])
    fine, mid = grid.level(1.0), grid.level(2.0)
    diag2 = 1.0 + 16.0 * c_ref[...]
    entry = ef_ref[...]
    x = halo_ref[0]
    rho0 = keep_ref[4] + x
    rho1 = keep_ref[5]
    m = (keep_ref[6] + entry) / diag2
    v0 = mid.S(rho0) + m
    v1 = mid.S(rho1) + m
    xs = mid.S(x)
    before = entry - (x + xs - mid.K(xs))
    q0 = v0 + mid.S(rho0 - mid.K(v0) + before)
    q1 = v1 + mid.S(rho1 - mid.K(v1) + v0)
    qb = halo_ref[1] + mid.S(mid.S(far_ref[...])) + mid.T(entry)
    ub = x + qb
    pb = halo_ref[2] + fine.T(qb)
    nine = [jnp.zeros((ROWS, LANES), jnp.float32) for _ in range(9)]
    q = (q0, q0, q1, q1)
    for t in range(4):
        u = keep_ref[t] + q[t]
        p = u + fine.S(r_ref[t] - fine.K(u) + ub)
        p_ref[t] = p
        w_ref[t] = fine.K(p) - pb
        ub, pb = u, p
    copy.wait()
    for t in range(4):
        for _, rows, cols in tiles(sx, sy):
            w = w_ref[t, rows, cols]
            for k in range(8):
                nine[k] = nine[k] + w * q_ref[k, t, rows, cols]
            nine[8] = nine[8] + w * w
    lane = lax.broadcasted_iota(jnp.int32, (ROWS, LANES), 1)
    out = jnp.zeros((ROWS, LANES), jnp.float32)
    for k in range(9):
        out = jnp.where(lane == k, jnp.sum(nine[k], axis=(0, 1), keepdims=True), out)
    for b in range(dots_ref.shape[0] // ROWS):
        dots_ref[b * ROWS : (b + 1) * ROWS, :] = out


def two_sum(a, b):
    total = a + b
    part = total - a
    return total, (a - (total - part)) + (b - part)


def two_square(a):
    big = a * 4097.0
    high = big - (big - a)
    low = a - high
    square = a * a
    return square, ((high * high - square) + 2.0 * high * low) + low * low


def pair_add(a, b):
    high, low = two_sum(a[0], b[0])
    return high, low + (a[1] + b[1])


def finish_kernel(cells, dots_ref, w_ref, q_hbm, next_ref, coef_ref, q_ref, sem):
    copy = pltpu.make_async_copy(q_hbm, q_ref, sem)
    copy.start()
    parts = [(dots_ref[b * ROWS : (b + 1) * ROWS, :], jnp.zeros((ROWS, LANES), jnp.float32)) for b in range(dots_ref.shape[0] // ROWS)]
    while len(parts) > 1:
        parts = [pair_add(parts[2 * i], parts[2 * i + 1]) for i in range(len(parts) // 2)]
    pair = parts[0]
    for by in (4, 2, 1):
        pair = pair_add(pair, (pltpu.roll(pair[0], by, 0), pltpu.roll(pair[1], by, 0)))
    high, low = two_sum(pair[0] / cells, pair[1] / cells)
    lane = lax.broadcasted_iota(jnp.int32, (ROWS, LANES), 1)
    sq, sq_low = two_square(high)
    is_h = lane < 8
    is_s = lane == 8
    zero = jnp.zeros_like(high)
    rest = (
        jnp.where(is_h, -sq, jnp.where(is_s, high, zero)),
        jnp.where(is_h, -(sq_low + 2.0 * high * low), jnp.where(is_s, low, zero)),
    )
    for by in (8, 4, 2, 1):
        rest = pair_add(rest, (pltpu.roll(rest[0], LANES - by, 1), pltpu.roll(rest[1], LANES - by, 1)))
    square = jnp.broadcast_to((rest[0] + rest[1])[:, 0:1], (ROWS, LANES))
    length = jnp.sqrt(jnp.maximum(square, 0.0))
    scale = 1.0 / jnp.maximum(length, FLOOR)
    coef = jnp.where(is_s, length, high)
    coef_ref[...] = coef[0, :9]
    h = [jnp.broadcast_to(high[:, k : k + 1], (ROWS, LANES)) for k in range(8)]
    copy.wait()
    steps, sx, sy = w_ref.shape
    for t in range(steps):
        for _, rows, cols in tiles(sx, sy):
            w = w_ref[t, rows, cols]
            for k in range(8):
                w = w - h[k] * q_ref[k, t, rows, cols]
            next_ref[t, rows, cols] = w * scale


def whole(n):
    return [pl.BlockSpec(memory_space=VMEM)] * n


def f32(*shape):
    return jax.ShapeDtypeStruct(shape, jnp.float32)


def on_device(krylov_basis, vector, conductance):
    count = lax.axis_size(TM)
    steps, sx, sy = vector.shape
    cells = float(steps * count * sx * sy)
    rows = sx * sy // LANES
    limit = pltpu.CompilerParams(vmem_limit_bytes=24 * 2**20)

    f, d, halo, x, keep = pl.pallas_call(
        down_kernel,
        out_shape=(f32(rows, LANES), f32(1, LANES), f32(3, sx, sy), f32(sx, sy), f32(7, sx, sy)),
        in_specs=whole(2),
        out_specs=tuple(whole(5)),
        scratch_shapes=[VMEM((rows, LANES), jnp.float32)],
        compiler_params=limit,
        name="down",
    )(vector, conductance)
    halo = lax.ppermute(halo, TM, [(k, k + 1) for k in range(count - 1)])
    far = lax.ppermute(x, TM, [(k, k + 2) for k in range(count - 2)])
    f = lax.all_to_all(f, TM, 0, 0, tiled=True)
    e = pl.pallas_call(
        scan_kernel,
        out_shape=f32(rows, LANES),
        in_specs=whole(2),
        out_specs=whole(1)[0],
        compiler_params=limit,
        name="scan",
    )(f, d)
    e = lax.all_to_all(e, TM, 0, 0, tiled=True)
    p, w, dots = pl.pallas_call(
        up_kernel,
        out_shape=(f32(steps, sx, sy), f32(steps, sx, sy), f32(count, LANES)),
        in_specs=whole(6) + [pl.BlockSpec(memory_space=pl.ANY)],
        out_specs=tuple(whole(3)),
        scratch_shapes=[
            VMEM(krylov_basis.shape, jnp.float32),
            VMEM((sx, sy), jnp.float32),
            pltpu.SemaphoreType.DMA,
        ],
        compiler_params=limit,
        name="up",
    )(e, vector, conductance, halo, far, keep, krylov_basis)
    dots = lax.all_to_all(dots, TM, 0, 0, tiled=True)
    following, coefficients = pl.pallas_call(
        functools.partial(finish_kernel, cells),
        out_shape=(f32(steps, sx, sy), f32(9)),
        in_specs=whole(2) + [pl.BlockSpec(memory_space=pl.ANY)],
        out_specs=tuple(whole(2)),
        scratch_shapes=[VMEM(krylov_basis.shape, jnp.float32), pltpu.SemaphoreType.DMA],
        compiler_params=limit,
        name="finish",
    )(dots, w, krylov_basis)
    return (p, following, coefficients)


def solution(mesh):
    return jax.shard_map(
        on_device,
        mesh=mesh,
        in_specs=(P(None, TM, None, None), P(TM, None, None), P()),
        out_specs=(P(TM, None, None), P(TM, None, None), P()),
        check_vma=False,
    )
```

time: 207 us -> 64.8 us (0.31)
  blocking collectives: 148 us -> 13.9 us
  starting transfers between devices: 34.2 us -> 22.1 us
  waiting for transfers between devices: 6.65 us -> 15.8 us
  matrix products: 8.17 us -> 0 us
  other arithmetic: 7.01 us -> 0 us
  Pallas kernels: 0 us -> 6.71 us
  local copies, waits for them, and re-layouts: 0.11 us -> 5.17 us
    psum x8 -> x0, blocking collectives: 76.6 us -> none  [by_axis(): return functools.reduce(lax.psum, axes, value)]
    all_gather x8 -> x0, blocking collectives: 71.7 us -> none  [carried_in(): pieces = jax.tree.map(lambda part: lax.all_gather(part, axis), subtotal)]
    ppermute x5 -> x2, starting transfers between devices: 34.2 us -> 7.75 us  [the longest x1 4.49 us: on_device(): halo = lax.ppermute(halo, TM, [(k, k + 1) for k in range(count - 1)])]
    all_to_all x0 -> x2, waiting for transfers between devices: none -> 15.8 us  [the longest x1 9.55 us: on_device(): e = lax.all_to_all(e, TM, 0, 0, tiled=True)]
    all_to_all x0 -> x2, starting transfers between devices: none -> 14.3 us  [the longest x1 9.82 us: on_device(): f = lax.all_to_all(f, TM, 0, 0, tiled=True)]
    all_to_all x0 -> x1, blocking collectives: none -> 13.9 us  [on_device(): dots = lax.all_to_all(dots, TM, 0, 0, tiled=True)]
    dot_general x2 -> x0, matrix products: 8.17 us -> none  [the longest x1 5.33 us: on_device(): jnp.einsum('kabc,abc->k', krylov_basis, applied, precision=lax.Precision....]
    pallas_call x0 -> x4, Pallas kernels: none -> 6.71 us  [the longest x1 2.99 us: on_device(): pl.pallas_call(up_kernel, out_shape=(f32(steps, sx, sy), f32(steps, sx, s...]
  transfers between devices with their start and end apart: 5 -> 4, of which waited for: 5 -> 2; matrix products, arithmetic and copies ran while one was open for 0% -> 0% of each run, Pallas kernels for 0% -> 1%
where the time goes in v1:
time: 64.8 us; the launch traced here: 64.4 us
  starting transfers between devices  22.1 us (34%)
  waiting for transfers between devices  15.8 us (24%)
  blocking collectives  13.9 us (21%)
  Pallas kernels  6.71 us (10%)
  local copies, waits for them, and re-layouts  5.17 us (8%)
  between operations  0.69 us (1%)
    all_to_all x1, blocking collectives, on_device(): dots = lax.all_to_all(dots, TM, 0, 0, tiled=True)  13.9 us
    all_to_all x1, starting transfers between devices, on_device(): f = lax.all_to_all(f, TM, 0, 0, tiled=True)  9.82 us
    all_to_all x1, waiting for transfers between devices, on_device(): e = lax.all_to_all(e, TM, 0, 0, tiled=True)  9.55 us
    all_to_all x1, waiting for transfers between devices, on_device(): f = lax.all_to_all(f, TM, 0, 0, tiled=True)  6.29 us
    unnamed x12, local copies, waits for them, and re-layouts  5.17 us
    all_to_all x1, starting transfers between devices, on_device(): e = lax.all_to_all(e, TM, 0, 0, tiled=True)  4.5 us
    ppermute x1, starting transfers between devices, on_device(): halo = lax.ppermute(halo, TM, [(k, k + 1) for k in range(count - 1)])  4.49 us
    ppermute x1, starting transfers between devices, on_device(): far = lax.ppermute(x, TM, [(k, k + 2) for k in range(count - 2)])  3.26 us
  transfers between devices with their start and end apart: 4, of which 2 were waited for; matrix products, arithmetic and copies ran while one was open for 0% of the time, Pallas kernels for 1%

profile of v1, /device:TPU:1, one launch (start us, length us, event | category | flops | bytes accessed | tf_op | source)
XLA Modules:
  0.0 64.4 jit_solution(7116379833403224665)
XLA Ops:
  0.6 0.0 copy-start.2
  0.6 0.9 %copy-done.2 = f32[4,32,512]{2,1,0:T(8,128)S(1)} copy-done((f32[4,32,512]{2,1,0:T(8,128)S(1)}, f32[4,32,512]{2,1,0:T(8,128)}, u32[]{:S(2)}) %copy-start.2) | copy-done | bytes 262168
  1.6 0.0 copy-start.4
  1.6 0.8 %copy-done.4 = f32[32,512]{1,0:T(8,128)S(1)} copy-done((f32[32,512]{1,0:T(8,128)S(1)}, f32[32,512]{1,0:T(8,128)}, u32[]{:S(2)}) %copy-start.4) | copy-done | bytes 65560
  2.4 1.6 %down.1 = (f32[128,128]{1,0:T(8,128)}, f32[1,128]{1,0:T(1,128)S(1)}, f32[3,32,512]{2,1,0:T(8,128)S(1)}, f32[32,512]{1,0:T(8,128)S(1)}, f32[7,32,512]{2,1,0:T(8,128)S(1)}) custom-call(f32[4,32,512]{2,1,0:T(8,128)S(1)} %copy-done.2, f32[32,512]{1,0:T(8,128)S(1)} %copy-done.4), custom_call_target="tpu_custom_call" | custom-call | tf_op jit(solution)/shard_map/down/pallas_call | solution.py:245
  4.1 4.5 %collective-permute-start = (f32[3,32,512]{2,1,0:T(8,128)S(1)}, f32[3,32,512]{2,1,0:T(8,128)S(1)}, u32[]{:S(2)}, u32[]{:S(2)}) collective-permute-start(f32[3,32,512]{2,1,0:T(8,128)S(1)} %get-tuple-element.15), channel_id=1, source_target_pairs={{0,1},{1,2},{2,3},{3,4},{4,5},{5,6},{6,7},{7,8},{8,9},{9,10},{10,1... | collective-permute-start | bytes 589832 | tf_op jit(solution)/shard_map/ppermute | solution.py:254
  8.6 9.8 %all-to-all-start = ((f32[128,1,128]{2,1,0:T(1,128)}), f32[128,1,128]{2,1,0:T(1,128)S(1)}, u32[]{:S(2)}, u32[]{:S(2)}) async-start(f32[128,1,128]{2,1,0:T(1,128)} %bitcast.1), calls=%async_computation | async-start | bytes 131072 | tf_op jit(solution)/shard_map/all_to_all | solution.py:256
  18.4 3.3 %collective-permute-start.1 = (f32[32,512]{1,0:T(8,128)S(1)}, f32[32,512]{1,0:T(8,128)S(1)}, u32[]{:S(2)}, u32[]{:S(2)}) collective-permute-start(f32[32,512]{1,0:T(8,128)S(1)} %get-tuple-element.16), channel_id=1, source_target_pairs={{0,2},{1,3},{2,4},{3,5},{4,6},{5,7},{6,8},{7,9},{8,10},{9,11},{10,... | collective-permute-start | bytes 196616 | tf_op jit(solution)/shard_map/ppermute | solution.py:255
  21.6 6.3 %all-to-all-done = f32[128,1,128]{2,1,0:T(1,128)S(1)} async-done(((f32[128,1,128]{2,1,0:T(1,128)}), f32[128,1,128]{2,1,0:T(1,128)S(1)}, u32[]{:S(2)}, u32[]{:S(2)}) %all-to-all-start) | async-done | bytes 65568 | tf_op jit(solution)/shard_map/all_to_all | solution.py:256
  27.9 0.7 %scan.1 = f32[128,128]{1,0:T(8,128)} custom-call(f32[128,128]{1,0:T(8,128)S(1)} %bitcast.14, f32[1,128]{1,0:T(1,128)S(1)} %get-tuple-element.14.d_ref), custom_call_target="tpu_custom_call" | custom-call | tf_op jit(solution)/shard_map/scan/pallas_call | solution.py:257
  28.6 4.5 %all-to-all-start.1 = ((f32[128,1,128]{2,1,0:T(1,128)}), f32[128,1,128]{2,1,0:T(1,128)S(1)}, u32[]{:S(2)}, u32[]{:S(2)}) async-start(f32[128,1,128]{2,1,0:T(1,128)} %bitcast.4), calls=%async_computation.1 | async-start | bytes 131072 | tf_op jit(solution)/shard_map/all_to_all | solution.py:265
  33.1 0.0 collective-permute-done.1.far_ref
  33.1 9.5 %all-to-all-done.1 = f32[128,1,128]{2,1,0:T(1,128)S(1)} async-done(((f32[128,1,128]{2,1,0:T(1,128)}), f32[128,1,128]{2,1,0:T(1,128)S(1)}, u32[]{:S(2)}, u32[]{:S(2)}) %all-to-all-start.1) | async-done | bytes 65568 | tf_op jit(solution)/shard_map/all_to_all | solution.py:265
  42.7 0.0 collective-permute-done.halo_ref
  42.7 0.0 copy-start
  42.7 1.6 %copy-done = f32[8,4,32,512]{3,2,1,0:T(8,128)S(1)} copy-done((f32[8,4,32,512]{3,2,1,0:T(8,128)S(1)}, f32[8,4,32,512]{3,2,1,0:T(8,128)}, u32[]{:S(2)}) %copy-start) | copy-done | bytes 2097176
  44.3 0.0 copy-start.3
  44.3 0.9 %copy-done.3 = f32[4,32,512]{2,1,0:T(8,128)S(1)} copy-done((f32[4,32,512]{2,1,0:T(8,128)S(1)}, f32[4,32,512]{2,1,0:T(8,128)}, u32[]{:S(2)}) %copy-start.3) | copy-done | bytes 262168
  45.2 0.0 copy-start.5
  45.2 0.8 %copy-done.5 = f32[32,512]{1,0:T(8,128)S(1)} copy-done((f32[32,512]{1,0:T(8,128)S(1)}, f32[32,512]{1,0:T(8,128)}, u32[]{:S(2)}) %copy-start.5) | copy-done | bytes 65560
  46.1 3.0 %up.1 = (f32[4,32,512]{2,1,0:T(8,128)}, f32[4,32,512]{2,1,0:T(8,128)S(1)}, f32[128,128]{1,0:T(8,128)S(1)}) custom-call(f32[128,128]{1,0:T(8,128)S(1)} %bitcast.12, f32[4,32,512]{2,1,0:T(8,128)S(1)} %copy-done.3, f32[32,512]{1,0:T(8,128)S(1)} %copy-done.5, f32[3,32,512]{2,1,0:T(8,128)S(1)} %collective-permute-done.halo_ref, ...), custom_call_target="tpu_custom_call" | custom-call | tf_op jit(solution)/shard_map/up/pallas_call | solution.py:266
  49.1 13.9 %all_to_all.33 = f32[128,1,128]{2,1,0:T(1,128)S(1)} all-to-all(f32[128,1,128]{2,1,0:T(1,128)S(1)} %bitcast.15), channel_id=1, replica_groups=mesh['tm'=128] {'tm'}, dimensions={0} | all-to-all | bytes 131072 | tf_op jit(solution)/shard_map/all_to_all | solution.py:279
  63.0 0.0 copy-done.1
  63.0 1.4 %finish.1 = (f32[4,32,512]{2,1,0:T(8,128)}, f32[9]{0:T(128)}) custom-call(f32[128,128]{1,0:T(8,128)S(1)} %bitcast.13, f32[4,32,512]{2,1,0:T(8,128)S(1)} %get-tuple-element.20.w_ref, f32[8,4,32,512]{3,2,1,0:T(8,128)S(1)} %copy-done.1), custom_call_target="tpu_custom_call" | custom-call | tf_op jit(solution)/shard_map/finish/pallas_call | solution.py:280
  (1 shorter events, 0.0 us)
Async XLA Ops:
  0.6 1.0 %copy-start.2 = (f32[4,32,512]{2,1,0:T(8,128)S(1)}, f32[4,32,512]{2,1,0:T(8,128)}, u32[]{:S(2)}) copy-start(f32[4,32,512]{2,1,0:T(8,128)} %r_ref.3) | copy-start | bytes 786436
  1.6 0.8 %copy-start.4 = (f32[32,512]{1,0:T(8,128)S(1)}, f32[32,512]{1,0:T(8,128)}, u32[]{:S(2)}) copy-start(f32[32,512]{1,0:T(8,128)} %c_ref.3) | copy-start | bytes 196612
  4.1 38.6 %collective-permute-start = (f32[3,32,512]{2,1,0:T(8,128)S(1)}, f32[3,32,512]{2,1,0:T(8,128)S(1)}, u32[]{:S(2)}, u32[]{:S(2)}) collective-permute-start(f32[3,32,512]{2,1,0:T(8,128)S(1)} %get-tuple-element.15), channel_id=1, source_target_pairs={{0,1},{1,2},{2,3},{3,4},{4,5},{5,6},{6,7},{7,8},{8,9},{9,10},{10,1... | collective-permute-start | bytes 589832 | tf_op jit(solution)/shard_map/ppermute | solution.py:254
  8.6 19.4 %all-to-all-start = ((f32[128,1,128]{2,1,0:T(1,128)}), f32[128,1,128]{2,1,0:T(1,128)S(1)}, u32[]{:S(2)}, u32[]{:S(2)}) async-start(f32[128,1,128]{2,1,0:T(1,128)} %bitcast.1), calls=%async_computation | async-start | bytes 131072 | tf_op jit(solution)/shard_map/all_to_all | solution.py:256
  18.4 14.7 %collective-permute-start.1 = (f32[32,512]{1,0:T(8,128)S(1)}, f32[32,512]{1,0:T(8,128)S(1)}, u32[]{:S(2)}, u32[]{:S(2)}) collective-permute-start(f32[32,512]{1,0:T(8,128)S(1)} %get-tuple-element.16), channel_id=1, source_target_pairs={{0,2},{1,3},{2,4},{3,5},{4,6},{5,7},{6,8},{7,9},{8,10},{9,11},{10,... | collective-permute-start | bytes 196616 | tf_op jit(solution)/shard_map/ppermute | solution.py:255
  28.6 14.1 %all-to-all-start.1 = ((f32[128,1,128]{2,1,0:T(1,128)}), f32[128,1,128]{2,1,0:T(1,128)S(1)}, u32[]{:S(2)}, u32[]{:S(2)}) async-start(f32[128,1,128]{2,1,0:T(1,128)} %bitcast.4), calls=%async_computation.1 | async-start | bytes 131072 | tf_op jit(solution)/shard_map/all_to_all | solution.py:265
  42.7 1.6 %copy-start = (f32[8,4,32,512]{3,2,1,0:T(8,128)S(1)}, f32[8,4,32,512]{3,2,1,0:T(8,128)}, u32[]{:S(2)}) copy-start(f32[8,4,32,512]{3,2,1,0:T(8,128)} %q_hbm.3) | copy-start | bytes 6291460
  44.3 0.9 %copy-start.3 = (f32[4,32,512]{2,1,0:T(8,128)S(1)}, f32[4,32,512]{2,1,0:T(8,128)}, u32[]{:S(2)}) copy-start(f32[4,32,512]{2,1,0:T(8,128)} %r_ref.3) | copy-start | bytes 786436
  45.2 0.8 %copy-start.5 = (f32[32,512]{1,0:T(8,128)S(1)}, f32[32,512]{1,0:T(8,128)}, u32[]{:S(2)}) copy-start(f32[32,512]{1,0:T(8,128)} %c_ref.3) | copy-start | bytes 196612
  46.1 16.9 %copy-start.1 = (f32[8,4,32,512]{3,2,1,0:T(8,128)S(1)}, f32[8,4,32,512]{3,2,1,0:T(8,128)}, u32[]{:S(2)}) copy-start(f32[8,4,32,512]{3,2,1,0:T(8,128)} %q_hbm.3) | copy-start | bytes 6291460

commit v2 on v1

v2 whole, which is shorter than its diff:
```python
import functools

import jax
import jax.numpy as jnp
from jax import lax
from jax.experimental import pallas as pl
from jax.experimental.pallas import tpu as pltpu
from jax.sharding import PartitionSpec as P


TM = "tm"
OMEGA = 0.7
FLOOR = 0.25
ROWS, LANES = 8, 128
VMEM = pltpu.VMEM


class Grid:
    def __init__(self, conduct):
        sx, sy = conduct.shape
        row = lax.broadcasted_iota(jnp.int32, (sx, sy), 0)
        col = lax.broadcasted_iota(jnp.int32, (sx, sy), 1)
        self.sx, self.sy = sx, sy
        self.first_row, self.last_row = row == 0, row == sx - 1
        self.first_col, self.last_col = col == 0, col == sy - 1
        self.conduct = conduct

    def beside(self, v):
        zero = jnp.zeros_like(v)
        above = jnp.where(self.first_row, zero, pltpu.roll(v, 1, 0))
        below = jnp.where(self.last_row, zero, pltpu.roll(v, self.sx - 1, 0))
        left = jnp.where(self.first_col, zero, pltpu.roll(v, 1, 1))
        right = jnp.where(self.last_col, zero, pltpu.roll(v, self.sy - 1, 1))
        return (above + below) + (left + right)

    def level(self, scale):
        return Level(self, scale)


class Level:
    def __init__(self, grid, scale):
        self.grid = grid
        self.c = scale * grid.conduct
        self.diag = 1.0 + 4.0 * self.c
        self.inv = 1.0 / self.diag
        self.winv = OMEGA * self.inv

    def K(self, v):
        return self.diag * v - self.c * self.grid.beside(v)

    def S(self, r):
        return (r + self.c * self.grid.beside(r * self.inv)) * self.winv

    def T(self, v):
        return v + self.S(v - self.K(v))


def tiles(sx, sy):
    for i in range(sx // ROWS):
        for l in range(sy // LANES):
            yield (i * (sy // LANES) + l), slice(ROWS * i, ROWS * (i + 1)), slice(LANES * l, LANES * (l + 1))


def every_other(tile, which):
    return pl.ds(2 * ROWS * tile + which, ROWS, stride=2)


def down_kernel(r_hbm, c_hbm, f_ref, d_ref, r_ref, c_ref, u_ref, keep_ref, mid_ref, ct_ref, sems):
    copies = [pltpu.make_async_copy(r_hbm, r_ref, sems.at[0]), pltpu.make_async_copy(c_hbm, c_ref, sems.at[1])]
    for copy in copies:
        copy.start()
    for copy in copies:
        copy.wait()
    sx, sy = c_ref.shape
    grid = Grid(c_ref[...])
    fine, mid = grid.level(1.0), grid.level(2.0)
    r = [r_ref[t] for t in range(4)]
    u = [fine.S(r[t]) for t in range(4)]
    for t in range(4):
        u_ref[t] = u[t]
    rho0 = r[0] + r[1] - fine.K(u[0] + u[1]) + u[0]
    rho1 = r[2] + r[3] - fine.K(u[2] + u[3]) + u[1] + u[2]
    v0 = mid.S(rho0)
    v1 = mid.S(rho1)
    xs = mid.S(u[3])
    g = u[3] + v1 + xs - mid.K(xs)
    part = (rho0 + rho1 - mid.K(v0 + v1) + v0) / (1.0 + 16.0 * grid.conduct)
    f = part + g
    xss = mid.S(xs)
    for t, rows, cols in tiles(sx, sy):
        f_ref[every_other(t, 0), :] = f[rows, cols]
        f_ref[every_other(t, 1), :] = xss[rows, cols]
        ct_ref[t * ROWS : (t + 1) * ROWS, :] = c_ref[rows, cols]
    me = lax.axis_index(TM)
    d_ref[...] = 1.0 / (1.0 + 16.0 * ct_ref[pl.ds(me, 1), :])
    for k, field in enumerate((rho0, rho1, part)):
        keep_ref[k] = field
    for k, field in enumerate((v0, v1, g)):
        mid_ref[k] = field


def halo_kernel(r_ref, c_ref, u_ref, keep_ref, mid_ref, halo_ref):
    grid = Grid(c_ref[...])
    fine, mid = grid.level(1.0), grid.level(2.0)
    x = u_ref[3]
    rho1, v0, v1 = keep_ref[1], mid_ref[0], mid_ref[1]
    halo_ref[0] = x
    halo_ref[1] = v1 + mid.S(rho1 - mid.K(v1) + v0) - mid.T(mid_ref[2])
    halo_ref[2] = x + fine.S(r_ref[3] - fine.K(x) + u_ref[2])


def early_kernel(r_hbm, c_ref, u_ref, keep_ref, halo_ref, q_hbm, p_ref, w_ref, q_ref, r_ref, sems):
    fetch = pltpu.make_async_copy(r_hbm, r_ref, sems.at[1])
    fetch.start()
    copy = pltpu.make_async_copy(q_hbm, q_ref, sems.at[0])
    copy.start()
    grid = Grid(c_ref[...])
    fine, mid = grid.level(1.0), grid.level(2.0)
    x = halo_ref[0]
    part = keep_ref[2]
    xs = mid.S(x)
    rho0, rho1 = keep_ref[0] + x, keep_ref[1]
    v0 = mid.S(rho0) + part
    v1 = mid.S(rho1) + part
    q0 = v0 + mid.S(rho0 - mid.K(v0) - (x + xs - mid.K(xs)))
    q1 = v1 + mid.S(rho1 - mid.K(v1) + v0)
    qb = halo_ref[1]
    ub = x + qb
    pb = halo_ref[2] + fine.T(qb)
    q = (q0, q0, q1, q1)
    fetch.wait()
    for t in range(4):
        u = u_ref[t] + q[t]
        p = u + fine.S(r_ref[t] - fine.K(u) + ub)
        p_ref[t] = p
        w_ref[t] = fine.K(p) - pb
        ub, pb = u, p
    copy.wait()


def scan_kernel(f_ref, d_ref, e_ref):
    count = f_ref.shape[0] // 2
    row = lax.broadcasted_iota(jnp.int32, (ROWS, LANES), 0)
    d1 = jnp.broadcast_to(d_ref[...], (ROWS, LANES))
    d2 = d1 * d1
    d4 = d2 * d2
    d8 = d4 * d4
    one = jnp.ones_like(d1)
    power = (
        jnp.where((row & 1) > 0, d1, one)
        * jnp.where((row & 2) > 0, d2, one)
        * jnp.where((row & 4) > 0, d4, one)
    )
    carry = jnp.zeros((ROWS, LANES), jnp.float32)

    def shifted(v, by):
        return jnp.where(row < by, 0.0, pltpu.roll(v, by, 0))

    blocks = []
    for b in range(count // ROWS):
        y = f_ref[every_other(b, 0), :]
        y = y + d1 * shifted(y, 1)
        y = y + d2 * shifted(y, 2)
        y = y + d4 * shifted(y, 4)
        blocks.append(y)
    for b, y in enumerate(blocks):
        e_ref[every_other(b, 0), :] = shifted(y, 1) + power * carry
        carry = jnp.broadcast_to(y[ROWS - 1 : ROWS, :], (ROWS, LANES)) + d8 * carry
    last = jnp.zeros((ROWS, LANES), jnp.float32)
    for b in range(count // ROWS):
        far = pltpu.roll(f_ref[every_other(b, 1), :], 2, 0)
        e_ref[every_other(b, 1), :] = jnp.where(row < 2, last, far)
        last = far


def up_kernel(e_ref, c_ref, pe_ref, we_ref, q_ref, p_ref, w_ref, dots_ref, ef_ref, far_ref):
    sx, sy = c_ref.shape
    for t, rows, cols in tiles(sx, sy):
        ef_ref[rows, cols] = e_ref[every_other(t, 0), :]
        far_ref[rows, cols] = e_ref[every_other(t, 1), :]
    grid = Grid(c_ref[...])
    fine, mid = grid.level(1.0), grid.level(2.0)
    entry = ef_ref[...]
    m = entry / (1.0 + 16.0 * grid.conduct)
    mk = mid.K(m)
    q0 = m + mid.S(entry - mk)
    q1 = m + mid.S(m - mk)
    qb = mid.T(entry) + far_ref[...]
    k0, k1 = fine.K(q0), fine.K(q1)
    before = qb + fine.S(qb - fine.K(qb))
    for t, base, source in ((0, q0, qb - k0), (1, q0, q0 - k0), (2, q1, q0 - k1), (3, q1, q1 - k1)):
        p = base + fine.S(source)
        p_ref[t] = pe_ref[t] + p
        w_ref[t] = we_ref[t] + (fine.K(p) - before)
        before = p
    nine = [jnp.zeros((ROWS, LANES), jnp.float32) for _ in range(9)]
    for t in range(4):
        for _, rows, cols in tiles(sx, sy):
            w = w_ref[t, rows, cols]
            for k in range(8):
                nine[k] = nine[k] + w * q_ref[k, t, rows, cols]
            nine[8] = nine[8] + w * w
    lane = lax.broadcasted_iota(jnp.int32, (ROWS, LANES), 1)
    out = jnp.zeros((ROWS, LANES), jnp.float32)
    for k in range(9):
        out = jnp.where(lane == k, jnp.sum(nine[k], axis=(0, 1), keepdims=True), out)
    for b in range(dots_ref.shape[0] // ROWS):
        dots_ref[b * ROWS : (b + 1) * ROWS, :] = out


def two_sum(a, b):
    total = a + b
    part = total - a
    return total, (a - (total - part)) + (b - part)


def two_square(a):
    big = a * 4097.0
    high = big - (big - a)
    low = a - high
    square = a * a
    return square, ((high * high - square) + 2.0 * high * low) + low * low


def pair_add(a, b):
    high, low = two_sum(a[0], b[0])
    return high, low + (a[1] + b[1])


def finish_kernel(cells, dots_ref, w_ref, q_ref, p_ref, p_hbm, next_hbm, coef_hbm, next_ref, coef_ref, sems):
    copies = [pltpu.make_async_copy(p_ref, p_hbm, sems.at[0])]
    copies[0].start()
    parts = [(dots_ref[b * ROWS : (b + 1) * ROWS, :], jnp.zeros((ROWS, LANES), jnp.float32)) for b in range(dots_ref.shape[0] // ROWS)]
    while len(parts) > 1:
        parts = [pair_add(parts[2 * i], parts[2 * i + 1]) for i in range(len(parts) // 2)]
    pair = parts[0]
    for by in (4, 2, 1):
        pair = pair_add(pair, (pltpu.roll(pair[0], by, 0), pltpu.roll(pair[1], by, 0)))
    high, low = two_sum(pair[0] / cells, pair[1] / cells)
    lane = lax.broadcasted_iota(jnp.int32, (ROWS, LANES), 1)
    sq, sq_low = two_square(high)
    is_h = lane < 8
    is_s = lane == 8
    zero = jnp.zeros_like(high)
    rest = (
        jnp.where(is_h, -sq, jnp.where(is_s, high, zero)),
        jnp.where(is_h, -(sq_low + 2.0 * high * low), jnp.where(is_s, low, zero)),
    )
    for by in (8, 4, 2, 1):
        rest = pair_add(rest, (pltpu.roll(rest[0], LANES - by, 1), pltpu.roll(rest[1], LANES - by, 1)))
    square = jnp.broadcast_to((rest[0] + rest[1])[:, 0:1], (ROWS, LANES))
    length = jnp.sqrt(jnp.maximum(square, 0.0))
    scale = 1.0 / jnp.maximum(length, FLOOR)
    coef = jnp.where(is_s, length, high)
    coef_ref[...] = coef[0, :9]
    copies.append(pltpu.make_async_copy(coef_ref, coef_hbm, sems.at[1]))
    copies[1].start()
    h = [jnp.broadcast_to(high[:, k : k + 1], (ROWS, LANES)) for k in range(8)]
    steps, sx, sy = w_ref.shape
    for t in range(steps):
        for _, rows, cols in tiles(sx, sy):
            w = w_ref[t, rows, cols]
            for k in range(8):
                w = w - h[k] * q_ref[k, t, rows, cols]
            next_ref[t, rows, cols] = w * scale
        copies.append(pltpu.make_async_copy(next_ref.at[t], next_hbm.at[t], sems.at[2 + t]))
        copies[-1].start()
    for copy in copies:
        copy.wait()


def f32(*shape):
    return jax.ShapeDtypeStruct(shape, jnp.float32)


def held(*shape):
    return pltpu.VMEM(shape, jnp.float32)


IN_HBM = pl.BlockSpec(memory_space=pltpu.HBM)
IN_VMEM = pl.BlockSpec(memory_space=VMEM)


def call(kernel, ins, outs, scratch=(), cost=2**21):
    def run(*args):
        args = [pltpu.with_memory_space_constraint(a, pltpu.HBM) if s is IN_HBM else a for a, s in zip(args, ins)]
        return pl.pallas_call(
            kernel,
            out_shape=tuple(shape for shape, _ in outs),
            in_specs=list(ins),
            out_specs=tuple(spec for _, spec in outs),
            scratch_shapes=list(scratch),
            compiler_params=pltpu.CompilerParams(vmem_limit_bytes=16 * 2**20),
            cost_estimate=pl.CostEstimate(flops=cost, bytes_accessed=2**20, transcendentals=0),
        )(*args)

    return run


def exchanged(value):
    count = lax.axis_size(TM)
    pieces = value.reshape(count, value.shape[0] // count, LANES)
    return lax.all_to_all(pieces, TM, 0, 0, tiled=True).reshape(value.shape)


def passed(value, by, count):
    return lax.ppermute(value, TM, [(k, k + by) for k in range(count - by)])


def on_device(krylov_basis, vector, conductance):
    count = lax.axis_size(TM)
    steps, sx, sy = vector.shape
    cells = float(steps * count * sx * sy)
    rows = sx * sy // LANES
    slab = held(steps, sx, sy)
    out = pltpu.HBM((steps, sx, sy), jnp.float32)
    dma = pltpu.SemaphoreType.DMA

    f, d, r, c, u, keep, mid = call(
        down_kernel,
        [IN_HBM] * 2,
        [
            (s, IN_VMEM)
            for s in (f32(2 * rows, LANES), held(1, LANES), slab, held(sx, sy), slab, held(3, sx, sy), held(3, sx, sy))
        ],
        [held(rows, LANES), dma((2,))],
    )(vector, conductance)
    f = exchanged(f)
    (halo,) = call(halo_kernel, [IN_VMEM] * 5, [(held(3, sx, sy), IN_VMEM)])(r, c, u, keep, mid)
    halo = passed(halo, 1, count)
    (e,) = call(scan_kernel, [IN_VMEM] * 2, [(f32(2 * rows, LANES), IN_VMEM)])(f, d)
    e = exchanged(e)
    pe, we, q = call(
        early_kernel,
        [IN_HBM] + [IN_VMEM] * 4 + [IN_HBM],
        [(slab, IN_VMEM), (slab, IN_VMEM), (held(*krylov_basis.shape), IN_VMEM)],
        [slab, dma((2,))],
    )(vector, c, u, keep, halo, krylov_basis)
    p, w, dots = call(
        up_kernel,
        [IN_VMEM] * 5,
        [(slab, IN_VMEM), (slab, IN_VMEM), (f32(count, LANES), IN_VMEM)],
        [held(sx, sy), held(sx, sy)],
    )(e, c, pe, we, q)
    dots = exchanged(dots)
    p, following, coefficients = call(
        functools.partial(finish_kernel, cells),
        [IN_VMEM] * 4,
        [(out, IN_HBM), (out, IN_HBM), (pltpu.HBM((9,), jnp.float32), IN_HBM)],
        [slab, held(9), dma((6,))],
    )(dots, w, q, p)
    return (p, following, coefficients)


def solution(mesh):
    return jax.shard_map(
        on_device,
        mesh=mesh,
        in_specs=(P(None, TM, None, None), P(TM, None, None), P()),
        out_specs=(P(TM, None, None), P(TM, None, None), P()),
        check_vma=False,
    )
```

time: 64.8 us -> 55.7 us (0.86)
  local copies, waits for them, and re-layouts: 5.17 us -> 0 us
  starting transfers between devices: 22.1 us -> 19.2 us
  waiting for transfers between devices: 15.8 us -> 14.1 us
  Pallas kernels: 6.71 us -> 7.79 us
    unnamed x12 -> x0, local copies, waits for them, and re-layouts: 5.17 us -> none
    ppermute x2 -> x1, starting transfers between devices: 7.75 us -> 3.54 us  [passed(): return lax.ppermute(value, TM, [(k, k + by) for k in range(count - by)])]
    all_to_all x2, waiting for transfers between devices: 15.8 us -> 14.1 us  [exchanged(): return lax.all_to_all(pieces, TM, 0, 0, tiled=True).reshape(value.shape)]
    all_to_all x2, starting transfers between devices: 14.3 us -> 15.7 us  [exchanged(): return lax.all_to_all(pieces, TM, 0, 0, tiled=True).reshape(value.shape)]
    pallas_call x4 -> x6, Pallas kernels: 6.71 us -> 7.79 us  [run(): pl.pallas_call(kernel, out_shape=tuple((shape for shape, _ in outs)), in_...]
  transfers between devices with their start and end apart: 4 -> 3, of which waited for: 2 -> 2; matrix products, arithmetic and copies ran while one was open for 0% -> 0% of each run, Pallas kernels for 1% -> 6%
where the time goes in v2:
time: 55.7 us; the launch traced here: 55.5 us
  starting transfers between devices  19.2 us (34%)
  waiting for transfers between devices  14.1 us (25%)
  blocking collectives  13.7 us (25%)
  Pallas kernels  7.79 us (14%)
  between operations  0.7 us (1%)
    all_to_all x2, starting transfers between devices, exchanged(): return lax.all_to_all(pieces, TM, 0, 0, tiled=True).reshape(value.shape)  15.7 us
    all_to_all x2, waiting for transfers between devices, exchanged(): return lax.all_to_all(pieces, TM, 0, 0, tiled=True).reshape(value.shape)  14.1 us
    all_to_all x1, blocking collectives, exchanged(): return lax.all_to_all(pieces, TM, 0, 0, tiled=True).reshape(value.shape)  13.7 us
    pallas_call x6, Pallas kernels, run(): pl.pallas_call(kernel, out_shape=tuple((shape for shape, _ in outs)), in_...  7.79 us
    ppermute x1, starting transfers between devices, passed(): return lax.ppermute(value, TM, [(k, k + by) for k in range(count - by)])  3.54 us
  transfers between devices with their start and end apart: 3, of which 2 were waited for; matrix products, arithmetic and copies ran while one was open for 0% of the time, Pallas kernels for 6%

profile of v2, /device:TPU:1, one launch (start us, length us, event | category | flops | bytes accessed | tf_op | source)
XLA Modules:
  0.0 55.5 jit_solution(13927884295111191177)
XLA Ops:
  0.6 2.3 %shard_map.58 = (f32[256,128]{1,0:T(8,128)}, f32[1,128]{1,0:T(1,128)S(1)}, f32[4,32,512]{2,1,0:T(8,128)S(1)}, f32[32,512]{1,0:T(8,128)S(1)}, f32[4,32,512]{2,1,0...) custom-call(f32[4,32,512]{2,1,0:T(8,128)} %r_hbm.3, f32[32,512]{1,0:T(8,128)} %c_hbm.1), custom_call_target="tpu_custom_call" | custom-call | flops 2097152 | bytes 1048576 | tf_op jit(solution)/shard_map/pallas_call | solution.py:287
  2.9 11.5 %all-to-all-start = ((f32[128,2,128]{2,1,0:T(2,128)}), f32[128,2,128]{2,1,0:T(2,128)S(1)}, u32[]{:S(2)}, u32[]{:S(2)}) async-start(f32[128,2,128]{2,1,0:T(2,128)} %bitcast), calls=%async_computation | async-start | bytes 262144 | tf_op jit(solution)/shard_map/all_to_all | solution.py:303
  14.4 0.5 shard_map.60
  14.9 3.5 %collective-permute-start = (f32[3,32,512]{2,1,0:T(8,128)S(1)}, f32[3,32,512]{2,1,0:T(8,128)S(1)}, u32[]{:S(2)}, u32[]{:S(2)}) collective-permute-start(f32[3,32,512]{2,1,0:T(8,128)S(1)} %shard_map.60), channel_id=1, source_target_pairs={{0,1},{1,2},{2,3},{3,4},{4,5},{5,6},{6,7},{7,8},{8,9},{9,10},{10,1... | collective-permute-start | bytes 589832 | tf_op jit(solution)/shard_map/ppermute | solution.py:307
  18.5 6.0 %all-to-all-done = f32[128,2,128]{2,1,0:T(2,128)S(1)} async-done(((f32[128,2,128]{2,1,0:T(2,128)}), f32[128,2,128]{2,1,0:T(2,128)S(1)}, u32[]{:S(2)}, u32[]{:S(2)}) %all-to-all-start) | async-done | bytes 131104 | tf_op jit(solution)/shard_map/all_to_all | solution.py:303
  24.5 0.7 %shard_map.59 = f32[256,128]{1,0:T(8,128)} custom-call(f32[256,128]{1,0:T(8,128)S(1)} %bitcast.9, f32[1,128]{1,0:T(1,128)S(1)} %get-tuple-element.17.d_ref), custom_call_target="tpu_custom_call" | custom-call | flops 2097152 | bytes 1048576 | tf_op jit(solution)/shard_map/pallas_call | solution.py:287
  25.2 4.2 %all-to-all-start.1 = ((f32[128,2,128]{2,1,0:T(2,128)}), f32[128,2,128]{2,1,0:T(2,128)S(1)}, u32[]{:S(2)}, u32[]{:S(2)}) async-start(f32[128,2,128]{2,1,0:T(2,128)} %bitcast.2), calls=%async_computation.1 | async-start | bytes 262144 | tf_op jit(solution)/shard_map/all_to_all | solution.py:303
  29.4 0.0 collective-permute-done.halo_ref
  29.4 1.9 %shard_map.61 = (f32[4,32,512]{2,1,0:T(8,128)S(1)}, f32[4,32,512]{2,1,0:T(8,128)S(1)}, f32[8,4,32,512]{3,2,1,0:T(8,128)S(1)}) custom-call(f32[4,32,512]{2,1,0:T(8,128)} %r_hbm.3, f32[32,512]{1,0:T(8,128)S(1)} %get-tuple-element.18.c_ref, f32[4,32,512]{2,1,0:T(8,128)S(1)} %get-tuple-element.19.u_ref, f32[3,32,512]{2,1,0:T(8,128)S(1)} %get-tuple-element.20.keep_ref, ...), custom_call_target="tpu_custom_call" | custom-call | flops 2097152 | bytes 1048576 | tf_op jit(solution)/shard_map/pallas_call | solution.py:287
  31.3 8.1 %all-to-all-done.1 = f32[128,2,128]{2,1,0:T(2,128)S(1)} async-done(((f32[128,2,128]{2,1,0:T(2,128)}), f32[128,2,128]{2,1,0:T(2,128)S(1)}, u32[]{:S(2)}, u32[]{:S(2)}) %all-to-all-start.1) | async-done | bytes 131104 | tf_op jit(solution)/shard_map/all_to_all | solution.py:303
  39.4 1.2 %shard_map.62 = (f32[4,32,512]{2,1,0:T(8,128)S(1)}, f32[4,32,512]{2,1,0:T(8,128)S(1)}, f32[128,128]{1,0:T(8,128)S(1)}) custom-call(f32[256,128]{1,0:T(8,128)S(1)} %bitcast.8, f32[32,512]{1,0:T(8,128)S(1)} %get-tuple-element.18.c_ref, f32[4,32,512]{2,1,0:T(8,128)S(1)} %get-tuple-element.23.pe_ref, f32[4,32,512]{2,1,0:T(8,128)S(1)} %get-tuple-element.24.we_ref, ...), custom_call_target="tpu_custom_call" | custom-call | flops 2097152 | bytes 1048576 | tf_op jit(solution)/shard_map/pallas_call | solution.py:287
  40.6 13.7 %all_to_all.15 = f32[128,1,128]{2,1,0:T(1,128)S(1)} all-to-all(f32[128,1,128]{2,1,0:T(1,128)S(1)} %bitcast.11), channel_id=1, replica_groups=mesh['tm'=128] {'tm'}, dimensions={0} | all-to-all | bytes 131072 | tf_op jit(solution)/shard_map/all_to_all | solution.py:303
  54.3 1.2 %shard_map.63 = (f32[4,32,512]{2,1,0:T(8,128)}, f32[4,32,512]{2,1,0:T(8,128)}, f32[9]{0:T(128)}) custom-call(f32[128,128]{1,0:T(8,128)S(1)} %bitcast.10, f32[4,32,512]{2,1,0:T(8,128)S(1)} %get-tuple-element.27.w_ref, f32[8,4,32,512]{3,2,1,0:T(8,128)S(1)} %get-tuple-element.25.q_ref, f32[4,32,512]{2,1,0:T(8,128)S(1)} %get-tuple-element.28.p_ref), custom_call_target="tpu_custom_call" | custom-call | flops 2097152 | bytes 1048576 | tf_op jit(solution)/shard_map/pallas_call | solution.py:287
Async XLA Ops:
  2.9 21.5 %all-to-all-start = ((f32[128,2,128]{2,1,0:T(2,128)}), f32[128,2,128]{2,1,0:T(2,128)S(1)}, u32[]{:S(2)}, u32[]{:S(2)}) async-start(f32[128,2,128]{2,1,0:T(2,128)} %bitcast), calls=%async_computation | async-start | bytes 262144 | tf_op jit(solution)/shard_map/all_to_all | solution.py:303
  14.9 14.5 %collective-permute-start = (f32[3,32,512]{2,1,0:T(8,128)S(1)}, f32[3,32,512]{2,1,0:T(8,128)S(1)}, u32[]{:S(2)}, u32[]{:S(2)}) collective-permute-start(f32[3,32,512]{2,1,0:T(8,128)S(1)} %shard_map.60), channel_id=1, source_target_pairs={{0,1},{1,2},{2,3},{3,4},{4,5},{5,6},{6,7},{7,8},{8,9},{9,10},{10,1... | collective-permute-start | bytes 589832 | tf_op jit(solution)/shard_map/ppermute | solution.py:307
  25.2 14.2 %all-to-all-start.1 = ((f32[128,2,128]{2,1,0:T(2,128)}), f32[128,2,128]{2,1,0:T(2,128)S(1)}, u32[]{:S(2)}, u32[]{:S(2)}) async-start(f32[128,2,128]{2,1,0:T(2,128)} %bitcast.2), calls=%async_computation.1 | async-start | bytes 262144 | tf_op jit(solution)/shard_map/all_to_all | solution.py:303
